TPU v7x, 128 devices: a whole 4x4x4 slice. The times are simulated.
128 devices in a mesh: rad: 8 (over z, x_lo), ang: 16 (over y, x_hi, core).
Axes of the slice: x: 4 (x_hi: 2, x_lo: 2; x = x_hi * 2 + x_lo), y: 4, z: 4, core: 2. Of those that a mesh axis runs over, the one named last changes fastest.
Arguments:
- state: float32 [4, 64, 512, 1024], P(None, 'rad', 'ang'), may hold values from -4 to 4, as said below
Outputs:
- increment: float32 [4, 64, 512, 1024], P(None, 'rad', 'ang')
- potential: float32 [64, 512, 1024], P('rad', 'ang')
Inputs may be any that keep to these rules, and one draw needn't show every extreme that they name: `state`: component 0 (density) lies between 0.5 and 2; components 1 to 3 (momentum) between -4 and 4.
All inputs are finite; a program needn't handle non-finite values.
Results may differ from a plain program's by a relative error of at most 0.0003.
Values sent between devices are 32-bit elements; how exact they have to be, the bound alone decides.
A program may use at most 192 MiB of HBM per device.

v0:
```python
import functools
import math

import jax
import jax.numpy as jnp
import numpy as np
from jax import lax
from jax.experimental import pallas as pl
from jax.experimental.pallas import tpu as pltpu
from jax.sharding import PartitionSpec as P

LMAX = 48
MPAD = 64
LANES = 128
NK = 56
GROUPS = 8
KD = 7
PADR = 8
WIDTH = 3
ROWS = 8

sound_speed = 0.5
sound_sq = 0.25
grav_const = 100.0
section_step = 0.001
inner_radius = 1.0
radial_span = 0.1
MESH = pl.DeviceIdType.MESH
f32 = jnp.float32
bf16 = jnp.bfloat16


def split_np(table):
    high = table.astype(bf16)
    low = (table - high.astype(np.float64)).astype(bf16)
    return high, low


def phi_tables(count):
    order = np.arange(MPAD, dtype=np.float64)
    norm = np.where(order > 0.5, math.sqrt(2.0), 1.0)
    phase = (2.0 * math.pi / count) * (np.outer(np.arange(count), np.arange(MPAD)) % count)
    table = np.concatenate([np.cos(phase) * norm, np.sin(phase) * norm], axis=1)
    high, low = split_np(table)
    back = np.concatenate([high.T, high.T, low.T], axis=0)
    step = 2.0 * math.pi / count
    slope = np.sin(order * step) / step
    return high, low, back, np.concatenate([slope, -slope])


def row_tables(blocks, rows):
    total = blocks * rows
    step_t = math.pi / total
    row = np.arange(blocks)[:, None] * rows + np.arange(rows + 2 * PADR)[None, :] - PADR
    theta = step_t * (row + 0.5)
    face = np.where((row > 0) & (row < total), np.sin(step_t * row), 0.0)
    table = np.zeros((blocks, rows + 2 * PADR, LANES))
    table[:, :, 0] = np.cos(theta)
    table[:, :, 1] = np.sin(theta)
    table[:, :, 2] = face
    return table.astype(np.float32)


def degree_tables(slope):
    m = np.arange(LANES) % MPAD
    k = np.arange(NK)[:, None]
    l = (m + k).astype(np.float64)
    alpha = np.zeros((NK, LANES))
    beta = np.zeros((NK, LANES))
    norm = np.full(LANES, 1.0 / math.sqrt(4.0 * math.pi))
    for q in range(1, MPAD):
        norm = np.where(m >= q, norm * math.sqrt((2.0 * q + 1.0) / (2.0 * q)), norm)
    alpha[0] = norm
    alpha[1:] = np.sqrt((4.0 * l[1:] ** 2 - 1.0) / (l[1:] ** 2 - m**2))
    beta[2:] = np.sqrt(((l[2:] - 1.0) ** 2 - m**2) / (4.0 * (l[2:] - 1.0) ** 2 - 1.0))
    alpha = np.where(l <= LMAX, alpha, 0.0)
    extra = np.zeros((8, LANES))
    extra[0] = slope
    return np.concatenate([alpha, beta, extra]).astype(np.float32)


def log_radii(blocks, shells):
    radius = inner_radius + radial_span / (blocks * shells) * (np.arange(blocks * shells) + 0.5)
    table = np.log(radius).reshape(blocks, shells, 1)
    return np.broadcast_to(table, (blocks, shells, LANES)).astype(np.float32)


def split(value):
    high = value.astype(bf16)
    return high, (value - high.astype(f32)).astype(bf16)


def dot(a, b):
    return jnp.dot(a, b, preferred_element_type=f32)


def flux(sums, jumps, component):
    inverse = 1.0 / sums[0]
    speed = sums[component] * inverse
    scaled = speed * (1.0 / 60.0)
    wave = 0.5 * (sound_speed + jnp.abs(speed))
    out = [s * scaled - wave * j for s, j in zip(sums, jumps)]
    out[component] = out[component] + (sound_sq / 60.0) * sums[0]
    return out


def kernel(
    n_rad,
    n_ang,
    shells,
    rows,
    cols,
    x_ref,
    fwd_high_ref,
    fwd_low_ref,
    back_ref,
    row_ref,
    degree_ref,
    log_ref,
    inc_ref,
    pot_ref,
    ext,
    lo,
    hi,
    tend,
    pot,
    fields,
    table,
    spec,
    rowtab,
    leg,
    partial,
    got_a,
    mine,
    got_b,
    tot_up,
    tot_down,
    got_up,
    got_down,
    coef,
    local_sem,
    out_sem,
    ang_send,
    ang_recv,
    rad_send,
    rad_recv,
    a_send,
    a_recv,
    b_send,
    b_recv,
    c_send,
    c_recv,
    d_send,
    d_recv,
):
    r = lax.axis_index("rad")
    a = lax.axis_index("ang")
    y, x_hi, core = a // 4, (a // 2) % 2, a % 2
    g = y * 2 + core
    chunks = rows // ROWS
    span = rows + 2 * PADR
    own = pl.ds(PADR, rows)
    step_r = radial_span / (n_rad * shells)
    step_t = math.pi / (n_ang * rows)
    step_p = 2.0 * math.pi / cols

    def peer(d):
        q = (g + d) % GROUPS
        return (r, (q // 2) * 4 + x_hi * 2 + q % 2)

    partner = (r, y * 4 + (1 - x_hi) * 2 + core)

    def when(cond, run):
        @pl.when(cond)
        def _():
            run()

    def remote(src, dst, send, recv, dev):
        return pltpu.make_async_remote_copy(
            src_ref=src,
            dst_ref=dst,
            send_sem=send,
            recv_sem=recv,
            device_id=dev,
            device_id_type=MESH,
        )

    load_density = pltpu.make_async_copy(x_ref.at[0], ext.at[0, :, own], local_sem.at[0])
    load_rest = pltpu.make_async_copy(
        x_ref.at[1:4], ext.at[1:4, :, own], local_sem.at[1]
    )
    load_rows = pltpu.make_async_copy(row_ref.at[a], rowtab, local_sem.at[2])
    load_density.start()
    load_rest.start()
    load_rows.start()

    got_up[...] = jnp.zeros_like(got_up)
    got_down[...] = jnp.zeros_like(got_down)

    @pl.when(a == 0)
    def _():
        ext[:, :, 0:PADR, :] = jnp.zeros((4, shells, PADR, cols), f32)

    @pl.when(a == n_ang - 1)
    def _():
        ext[:, :, PADR + rows : span, :] = jnp.zeros((4, shells, PADR, cols), f32)

    @pl.when(r == 0)
    def _():
        lo[...] = jnp.zeros_like(lo)

    @pl.when(r == n_rad - 1)
    def _():
        hi[...] = jnp.zeros_like(hi)

    barrier = pltpu.get_barrier_semaphore()

    def greet(cond, dev):
        when(
            cond,
            lambda: pl.semaphore_signal(barrier, inc=1, device_id=dev, device_id_type=MESH),
        )

    for d in range(1, n_rad):
        greet(r + d < n_rad, (r + d, a))
        greet(r - d >= 0, (r - d, a))
    for d in range(1, GROUPS):
        pl.semaphore_signal(barrier, inc=1, device_id=peer(d), device_id_type=MESH)
    pl.semaphore_signal(barrier, inc=1, device_id=partner, device_id_type=MESH)
    greet(a + 1 < n_ang, (r, a + 1))
    greet(a > 0, (r, a - 1))
    ends = jnp.where(a > 0, 1, 0) + jnp.where(a + 1 < n_ang, 1, 0)

    pl.semaphore_wait(barrier, n_rad - 1 + GROUPS + ends)

    ang_up = remote(
        x_ref.at[:, :, rows - WIDTH : rows],
        ext.at[:, :, PADR - WIDTH : PADR],
        ang_send.at[0],
        ang_recv.at[0],
        (r, a + 1),
    )
    ang_down = remote(
        x_ref.at[:, :, 0:WIDTH],
        ext.at[:, :, PADR + rows : PADR + rows + WIDTH],
        ang_send.at[1],
        ang_recv.at[1],
        (r, a - 1),
    )
    rad_up = []
    rad_down = []
    for c in range(chunks):
        part = pl.ds(c * ROWS, ROWS)
        rad_up.append(
            remote(
                x_ref.at[:, shells - WIDTH : shells, part],
                lo.at[:, :, part],
                rad_send.at[0, c],
                rad_recv.at[0, c],
                (r + 1, a),
            )
        )
        rad_down.append(
            remote(
                x_ref.at[:, 0:WIDTH, part],
                hi.at[:, :, part],
                rad_send.at[1, c],
                rad_recv.at[1, c],
                (r - 1, a),
            )
        )

    def start_chunk(c):
        when(r + 1 < n_rad, rad_up[c].start)
        when(r > 0, rad_down[c].start)

    when(a + 1 < n_ang, ang_up.start)
    when(a > 0, ang_down.start)
    start_chunk(0)

    load_rows.wait()
    cosine = jnp.broadcast_to(rowtab[:, 0:1], (span, LANES))
    sine = jnp.broadcast_to(rowtab[:, 1:2], (span, LANES))
    order = lax.broadcasted_iota(jnp.int32, (span, LANES), 1) % MPAD
    power = jnp.full((span, LANES), 1.0, f32)
    square = sine
    for bit in range(6):
        power = jnp.where((order // (1 << bit)) % 2 == 1, power * square, power)
        square = square * square
    level = power * degree_ref[0:1, :]
    leg[0] = level

    def next_level(k, carry):
        last, before = carry
        alpha = degree_ref[pl.ds(k, 1), :]
        beta = degree_ref[pl.ds(NK + k, 1), :]
        new = alpha * (cosine * last - beta * before)
        leg[k] = new
        return (new, last)

    lax.fori_loop(1, NK, next_level, (level, jnp.zeros_like(level)))

    load_density.wait()
    weight = sine[PADR : PADR + rows] * (step_t * step_p)
    half = shells // 2
    for h in range(2):
        cells = ext[0, h * half : (h + 1) * half, PADR : PADR + rows, :]
        high, low = split(cells.reshape(half * rows, cols))
        sums = dot(high, fwd_high_ref[...]) + (
            dot(low, fwd_high_ref[...]) + dot(high, fwd_low_ref[...])
        )
        for q in range(half):
            spec[pl.ds((h * half + q) * rows, rows), :] = (
                sums[q * rows : (q + 1) * rows] * weight
            )
    spectra = [spec[pl.ds(j, shells, stride=rows), :] for j in range(rows)]

    def moment(k, carry):
        parts = [jnp.zeros((shells, LANES), f32) for _ in range(4)]
        for j in range(rows):
            parts[j % 4] = parts[j % 4] + spectra[j] * leg[k, PADR + j : PADR + j + 1, :]
        partial[k // KD, k % KD] = (parts[0] + parts[1]) + (parts[2] + parts[3])
        return carry

    lax.fori_loop(0, NK, moment, 0)

    def exchange_a(d):
        return remote(
            partial.at[(g + d) % GROUPS], got_a.at[d], a_send.at[d], a_recv.at[d], peer(d)
        )

    for d in range(1, GROUPS):
        exchange_a(d).start()

    load_rest.wait()

    def phi_flux(index, carry):
        i = index // chunks
        at = pl.multiple_of((index % chunks) * ROWS, ROWS)
        cell_radius = inner_radius + step_r * ((r * shells + i).astype(f32) + 0.5)
        sums, jumps = [], []
        for c in range(4):
            u = ext[c, i, pl.ds(PADR + at, ROWS), :]
            left = pltpu.roll(u, 1, 1)
            near = u + left
            mid = pltpu.roll(u, cols - 1, 1) + pltpu.roll(u, 2, 1)
            far = pltpu.roll(u, cols - 2, 1) + pltpu.roll(u, 3, 1)
            sums.append(37.0 * near - 8.0 * mid + far)
            jumps.append(u - left)
        for c, face in enumerate(flux(sums, jumps, 3)):
            tend[c, i, pl.ds(at, ROWS), :] = (face - pltpu.roll(face, cols - 1, 1)) * (
                cell_radius / step_p
            )
        return carry

    lax.fori_loop(0, shells * chunks // 2, phi_flux, 0)

    for d in range(1, GROUPS):
        exchange_a(d).wait_recv()
    total = partial[g]
    for d in range(1, GROUPS):
        total = total + got_a[d]
    mine[...] = total
    exchange_b = remote(mine, got_b, b_send.at[0], b_recv.at[0], partner)
    exchange_b.start()
    start_chunk(1)

    lax.fori_loop(shells * chunks // 2, shells * chunks, phi_flux, 0)

    when(a > 0, ang_up.wait_recv)
    when(a + 1 < n_ang, ang_down.wait_recv)
    tiles = cols // LANES

    def theta_flux(index, carry):
        i = index // tiles
        lanes = pl.ds(pl.multiple_of((index % tiles) * LANES, LANES), LANES)
        cell_radius = inner_radius + step_r * ((r * shells + i).astype(f32) + 0.5)
        area = jnp.broadcast_to(rowtab[:, 2:3], (span, LANES)) * (cell_radius / step_t)
        sums, jumps = [], []
        for c in range(4):
            u = ext[c, i, :, lanes]
            left = pltpu.roll(u, 1, 0)
            near = u + left
            mid = pltpu.roll(u, span - 1, 0) + pltpu.roll(u, 2, 0)
            far = pltpu.roll(u, span - 2, 0) + pltpu.roll(u, 3, 0)
            sums.append(37.0 * near - 8.0 * mid + far)
            jumps.append(u - left)
        for c, face in enumerate(flux(sums, jumps, 2)):
            face = face * area
            change = face - pltpu.roll(face, span - 1, 0)
            tend[c, i, :, lanes] = tend[c, i, :, lanes] + change[PADR : PADR + rows]
        return carry

    lax.fori_loop(0, shells * tiles // 2, theta_flux, 0)

    exchange_b.wait_recv()
    total = mine[...] + got_b[...]
    log_radius = log_ref[r]
    shell = lax.broadcasted_iota(jnp.int32, (shells, LANES), 0)
    radius = inner_radius + step_r * ((r * shells + shell).astype(f32) + 0.5)
    order = lax.broadcasted_iota(jnp.int32, (shells, LANES), 1) % MPAD
    ups, downs, powers, degrees = [], [], [], []
    for q in range(KD):
        degree = (order + (g * KD + q)).astype(f32)
        grow = jnp.exp(degree * log_radius)
        weighted = (radius * radius * step_r) * total[q]
        up = grow * weighted
        down = weighted / (radius * grow)
        for s in (1, 2, 4):
            up = up + jnp.where(shell >= s, pltpu.roll(up, s, 0), 0.0)
            down = down + jnp.where(shell >= s, pltpu.roll(down, s, 0), 0.0)
        tot_up[q : q + 1, :] = up[shells - 1 : shells]
        tot_down[q : q + 1, :] = down[shells - 1 : shells]
        ups.append(up)
        downs.append(down)
        powers.append(grow)
        degrees.append(degree)

    def exchange_up(d):
        return remote(tot_up, got_up.at[d], c_send.at[0, d], c_recv.at[0, d], (r + d, a))

    def exchange_down(d):
        return remote(tot_down, got_down.at[d], c_send.at[1, d], c_recv.at[1, d], (r - d, a))

    for d in range(1, n_rad):
        when(r + d < n_rad, exchange_up(d).start)
        when(r - d >= 0, exchange_down(d).start)
    start_chunk(2)

    lax.fori_loop(shells * tiles // 2, shells * tiles, theta_flux, 0)

    for d in range(1, n_rad):
        when(r - d >= 0, exchange_up(d).wait_recv)
        when(r + d < n_rad, exchange_down(d).wait_recv)
    below = got_up[1]
    above = got_down[1]
    for d in range(2, n_rad):
        below = below + got_up[d]
        above = above + got_down[d]
    inverse_radius = 1.0 / radius
    for q in range(KD):
        inner = below[q : q + 1] + ups[q]
        outer = above[q : q + 1] + (downs[q][shells - 1 : shells] - downs[q])
        degree = degrees[q]
        norm = (-4.0 * math.pi) / (2.0 * degree + 1.0)
        inner_term = inner * inverse_radius / powers[q]
        outer_term = powers[q] * outer
        coef[g, 0, q] = norm * (inner_term + outer_term)
        coef[g, 1, q] = (
            norm * (degree * outer_term - (degree + 1.0) * inner_term) * inverse_radius
        )

    def exchange_d(d):
        return remote(coef.at[g], coef.at[g], d_send.at[d], d_recv.at[d], peer(d))

    for d in range(1, GROUPS):
        exchange_d(d).start()
    start_chunk(3)
    for d in range(1, GROUPS):
        exchange_d(d).wait_recv()

    slope_row = degree_ref[2 * NK : 2 * NK + 1, :]
    theta_scale = 1.0 / (2.0 * step_t)
    for i in range(0, shells, 2):

        def synthesize(h, carry):
            sums = list(carry)
            for q in range(KD):
                k = h * KD + q
                full = leg[k]
                value = full[PADR : PADR + rows]
                change = pltpu.roll(full, span - 1, 0) - pltpu.roll(full, 1, 0)
                change = change[PADR : PADR + rows]
                for p in range(2):
                    cp = coef[h, 0, q, i + p : i + p + 1, :]
                    cs = coef[h, 1, q, i + p : i + p + 1, :]
                    sums[3 * p] = sums[3 * p] + value * cp
                    sums[3 * p + 1] = sums[3 * p + 1] + value * cs
                    sums[3 * p + 2] = sums[3 * p + 2] + change * cp
            return tuple(sums)

        zero = jnp.zeros((rows, LANES), f32)
        sums = lax.fori_loop(0, (LMAX + KD) // KD, synthesize, (zero,) * 6)
        for p in range(2):
            base, slope, change = sums[3 * p : 3 * p + 3]
            at = (i + p) * 4 * rows
            table[at : at + rows, :] = base
            table[at + rows : at + 2 * rows, :] = slope
            table[at + 2 * rows : at + 3 * rows, :] = change * theta_scale
            table[at + 3 * rows : at + 4 * rows, :] = pltpu.roll(base, MPAD, 1) * slope_row

    def sources(i, carry):
        at = pl.multiple_of(i * 4 * rows, 4 * rows)
        high, low = split(table[pl.ds(at, 4 * rows), :])
        fields[...] = dot(jnp.concatenate([high, low, high], axis=1), back_ref[...])
        pot[i] = fields[0:rows, :]
        cell_radius = inner_radius + step_r * ((r * shells + i).astype(f32) + 0.5)
        for c in range(chunks):
            at = c * ROWS
            inside = pl.ds(PADR + at, ROWS)
            sine = jnp.broadcast_to(rowtab[inside, 1:2], (ROWS, cols)) * cell_radius
            cosine = jnp.broadcast_to(rowtab[inside, 0:1], (ROWS, cols)) * cell_radius
            density = ext[0, i, inside, :]
            mom_r = ext[1, i, inside, :]
            mom_t = ext[2, i, inside, :]
            mom_p = ext[3, i, inside, :]
            inverse = 1.0 / density
            vel_t = mom_t * inverse
            vel_p = mom_p * inverse
            pull = grav_const * density
            slope = fields[rows + at : rows + at + ROWS, :]
            grad_t = fields[2 * rows + at : 2 * rows + at + ROWS, :]
            grad_p = fields[3 * rows + at : 3 * rows + at + ROWS, :]
            twist = mom_p * vel_p
            source_r = sine * (
                (mom_t * vel_t + twist)
                + (2.0 * sound_sq) * density
                - (cell_radius * pull) * slope
            )
            source_t = cosine * (twist + sound_sq * density) - sine * (
                mom_r * vel_t + pull * grad_t
            )
            source_p = -(
                vel_p * (mom_r * sine + mom_t * cosine) + (cell_radius * pull) * grad_p
            )
            spot = pl.ds(at, ROWS)
            tend[1, i, spot, :] = tend[1, i, spot, :] + source_r
            tend[2, i, spot, :] = tend[2, i, spot, :] + source_t
            tend[3, i, spot, :] = tend[3, i, spot, :] + source_p
        return carry

    lax.fori_loop(0, shells, sources, 0)
    store_pot = pltpu.make_async_copy(pot, pot_ref, out_sem.at[chunks])
    store_pot.start()

    stores = []
    for chunk in range(chunks):
        when(r > 0, rad_up[chunk].wait_recv)
        when(r + 1 < n_rad, rad_down[chunk].wait_recv)
        at = chunk * ROWS
        spot = pl.ds(at, ROWS)

        def radial_flux(tile, carry):
            lanes = pl.ds(pl.multiple_of(tile * LANES, LANES), LANES)
            sine = jnp.broadcast_to(
                rowtab[PADR + at : PADR + at + ROWS, 1:2], (ROWS, LANES)
            ) * (section_step / step_r)

            def cell(c, s):
                if s < 0:
                    return lo[c, s + WIDTH, spot, lanes]
                if s >= shells:
                    return hi[c, s - shells, spot, lanes]
                return ext[c, s, pl.ds(PADR + at, ROWS), lanes]

            u = [[cell(c, s) for s in range(-WIDTH, shells + WIDTH)] for c in range(4)]
            last = None
            for f in range(shells + 1):
                place = r * shells + f
                face_radius = inner_radius + step_r * place.astype(f32)
                area = jnp.where(
                    (place > 0) & (place < n_rad * shells), face_radius * face_radius, 0.0
                )
                sums, jumps = [], []
                for c in range(4):
                    w = u[c][f : f + 6]
                    sums.append(37.0 * (w[2] + w[3]) - 8.0 * (w[1] + w[4]) + (w[0] + w[5]))
                    jumps.append(w[3] - w[2])
                face = [value * area for value in flux(sums, jumps, 1)]
                if f > 0:
                    for c in range(4):
                        tend[c, f - 1, spot, lanes] = (
                            section_step * tend[c, f - 1, spot, lanes]
                            - (face[c] - last[c]) * sine
                        )
                last = face
            return carry

        lax.fori_loop(0, tiles, radial_flux, 0)
        store = pltpu.make_async_copy(
            tend.at[:, :, spot], inc_ref.at[:, :, spot], out_sem.at[chunk]
        )
        store.start()
        stores.append(store)

    when(a + 1 < n_ang, ang_up.wait_send)
    when(a > 0, ang_down.wait_send)
    for c in range(chunks):
        when(r + 1 < n_rad, rad_up[c].wait_send)
        when(r > 0, rad_down[c].wait_send)
    for d in range(1, GROUPS):
        exchange_a(d).wait_send()
        exchange_d(d).wait_send()
    exchange_b.wait_send()
    for d in range(1, n_rad):
        when(r + d < n_rad, exchange_up(d).wait_send)
        when(r - d >= 0, exchange_down(d).wait_send)
    store_pot.wait()
    for store in stores:
        store.wait()


def solution(mesh):
    n_rad = mesh.shape["rad"]
    n_ang = mesh.shape["ang"]

    def body(state):
        _, shells, rows, cols = state.shape
        high, low, back, slope = phi_tables(cols)
        operands = (
            state,
            jnp.asarray(high),
            jnp.asarray(low),
            jnp.asarray(back),
            jnp.asarray(row_tables(n_ang, rows)),
            jnp.asarray(degree_tables(slope)),
            jnp.asarray(log_radii(n_rad, shells)),
        )
        span = rows + 2 * PADR
        chunks = rows // ROWS
        anywhere = pl.BlockSpec(memory_space=pl.ANY)
        inside = pl.BlockSpec(memory_space=pltpu.VMEM)
        dma = pltpu.SemaphoreType.DMA
        increment, potential = pl.pallas_call(
            functools.partial(kernel, n_rad, n_ang, shells, rows, cols),
            out_shape=(
                jax.ShapeDtypeStruct(state.shape, f32),
                jax.ShapeDtypeStruct(state.shape[1:], f32),
            ),
            in_specs=[anywhere, inside, inside, inside, anywhere, inside, inside],
            out_specs=(anywhere, anywhere),
            scratch_shapes=[
                pltpu.VMEM((4, shells, span, cols), f32),
                pltpu.VMEM((4, WIDTH, rows, cols), f32),
                pltpu.VMEM((4, WIDTH, rows, cols), f32),
                pltpu.VMEM((4, shells, rows, cols), f32),
                pltpu.VMEM((shells, rows, cols), f32),
                pltpu.VMEM((4 * rows, cols), f32),
                pltpu.VMEM((shells * 4 * rows, LANES), f32),
                pltpu.VMEM((shells * rows, LANES), f32),
                pltpu.VMEM((span, LANES), f32),
                pltpu.VMEM((NK, span, LANES), f32),
                pltpu.VMEM((GROUPS, KD, shells, LANES), f32),
                pltpu.VMEM((GROUPS, KD, shells, LANES), f32),
                pltpu.VMEM((KD, shells, LANES), f32),
                pltpu.VMEM((KD, shells, LANES), f32),
                pltpu.VMEM((8, LANES), f32),
                pltpu.VMEM((8, LANES), f32),
                pltpu.VMEM((n_rad, 8, LANES), f32),
                pltpu.VMEM((n_rad, 8, LANES), f32),
                pltpu.VMEM((GROUPS, 2, KD, shells, LANES), f32),
                dma((3,)),
                dma((chunks + 1,)),
                dma((2,)),
                dma((2,)),
                dma((2, chunks)),
                dma((2, chunks)),
                dma((GROUPS,)),
                dma((GROUPS,)),
                dma((1,)),
                dma((1,)),
                dma((2, n_rad)),
                dma((2, n_rad)),
                dma((GROUPS,)),
                dma((GROUPS,)),
            ],
            compiler_params=pltpu.CompilerParams(
                collective_id=0, has_side_effects=True, vmem_limit_bytes=56 << 20
            ),
        )(*operands)
        return increment, potential

    return jax.shard_map(
        body,
        mesh=mesh,
        in_specs=(P(None, "rad", "ang", None),),
        out_specs=(P(None, "rad", "ang", None), P("rad", "ang", None)),
        check_vma=False,
    )
```

profile of v0, /device:TPU:38, one launch (start us, length us, event | category | flops | bytes accessed | tf_op | source)
XLA Modules:
  0.0 94.1 jit_solution(14442515717663423200)
XLA Ops:
  0.6 87.6 %shard_map.86 = (f32[4,8,32,1024]{3,2,1,0:T(8,128)}, f32[8,32,1024]{2,1,0:T(8,128)}) custom-call(f32[4,8,32,1024]{3,2,1,0:T(8,128)} %x_ref.1, bf16[1024,128]{1,0:T(8,128)(2,1)} %constant.12.clone.fwd_high_ref, bf16[1024,128]{1,0:T(8,128)(2,1)} %constant.13.clone.fwd_low_ref, bf16[384,1024]{1,0:T(8,128)(2,1)} %constant.14.clone.back_ref, ...), custom_call_target="tpu_custom_call" | custom-call | tf_op jit(solution)/shard_map/pallas_call | solution.py:624
  88.2 0.0 copy-start
  88.2 4.9 %copy.11 = f32[4,8,32,1024]{3,2,1,0:T(8,128)} copy(f32[4,8,32,1024]{3,2,1,0:T(8,128)} %get-tuple-element.4) | data formatting | bytes 8388608
  93.1 0.0 copy-done
  93.1 1.0 %copy.12 = f32[8,32,1024]{2,1,0:T(8,128)} copy(f32[8,32,1024]{2,1,0:T(8,128)S(1)} %copy-done) | data formatting | bytes 2097152
Async XLA Ops:
  88.2 4.9 %copy-start = (f32[8,32,1024]{2,1,0:T(8,128)S(1)}, f32[8,32,1024]{2,1,0:T(8,128)}, u32[]{:S(2)}) copy-start(f32[8,32,1024]{2,1,0:T(8,128)} %get-tuple-element.5) | copy-start | bytes 3145732
where the time goes:
time: 94.2 us; the launch traced here: 94.1 us
  Pallas kernels  87.6 us (93%)
  local copies, waits for them, and re-layouts  5.85 us (6%)
    pallas_call x1, Pallas kernels, body(): pl.pallas_call(functools.partial(kernel, n_rad, n_ang, shells, rows, cols...  87.6 us
    unnamed x4, local copies, waits for them, and re-layouts  5.85 us

commit v1 on v0

--- a/solution.py
+++ b/solution.py
@@ -111,23 +111,27 @@
     rows,
     cols,
     x_ref,
+    fwd_high_hbm,
+    fwd_low_hbm,
+    back_hbm,
+    row_hbm,
+    degree_hbm,
+    log_hbm,
+    tend,
+    pot,
+    ext,
+    lo,
+    hi,
+    relay,
+    fields,
+    table,
+    spec,
     fwd_high_ref,
     fwd_low_ref,
     back_ref,
-    row_ref,
+    rowtab,
     degree_ref,
     log_ref,
-    inc_ref,
-    pot_ref,
-    ext,
-    lo,
-    hi,
-    tend,
-    pot,
-    fields,
-    table,
-    spec,
-    rowtab,
     leg,
     partial,
     got_a,
@@ -139,11 +143,12 @@
     got_down,
     coef,
     local_sem,
-    out_sem,
     ang_send,
     ang_recv,
     rad_send,
     rad_recv,
+    far_recv,
+    pass_send,
     a_send,
     a_recv,
     b_send,
@@ -189,30 +194,12 @@
     load_rest = pltpu.make_async_copy(
         x_ref.at[1:4], ext.at[1:4, :, own], local_sem.at[1]
     )
-    load_rows = pltpu.make_async_copy(row_ref.at[a], rowtab, local_sem.at[2])
-    load_density.start()
-    load_rest.start()
-    load_rows.start()
-
-    got_up[...] = jnp.zeros_like(got_up)
-    got_down[...] = jnp.zeros_like(got_down)
-
-    @pl.when(a == 0)
-    def _():
-        ext[:, :, 0:PADR, :] = jnp.zeros((4, shells, PADR, cols), f32)
-
-    @pl.when(a == n_ang - 1)
-    def _():
-        ext[:, :, PADR + rows : span, :] = jnp.zeros((4, shells, PADR, cols), f32)
-
-    @pl.when(r == 0)
-    def _():
-        lo[...] = jnp.zeros_like(lo)
-
-    @pl.when(r == n_rad - 1)
-    def _():
-        hi[...] = jnp.zeros_like(hi)
-
+    load_rows = pltpu.make_async_copy(row_hbm.at[a], rowtab, local_sem.at[2])
+    load_degree = pltpu.make_async_copy(degree_hbm, degree_ref, local_sem.at[3])
+    load_high = pltpu.make_async_copy(fwd_high_hbm, fwd_high_ref, local_sem.at[4])
+    load_low = pltpu.make_async_copy(fwd_low_hbm, fwd_low_ref, local_sem.at[5])
+    load_log = pltpu.make_async_copy(log_hbm.at[r], log_ref, local_sem.at[6])
+    load_back = pltpu.make_async_copy(back_hbm, back_ref, local_sem.at[7])
     barrier = pltpu.get_barrier_semaphore()
 
     def greet(cond, dev):
@@ -231,6 +218,10 @@
     greet(a > 0, (r, a - 1))
     ends = jnp.where(a > 0, 1, 0) + jnp.where(a + 1 < n_ang, 1, 0)
 
+    for load in (load_rows, load_degree, load_density, load_high, load_low):
+        load.start()
+    for load in (load_rest, load_log, load_back):
+        load.start()
     pl.semaphore_wait(barrier, n_rad - 1 + GROUPS + ends)
 
     ang_up = remote(
@@ -247,38 +238,82 @@
         ang_recv.at[1],
         (r, a - 1),
     )
-    rad_up = []
-    rad_down = []
+    rad_up, rad_down, far_up, far_down, pass_up, pass_down = [], [], [], [], [], []
     for c in range(chunks):
         part = pl.ds(c * ROWS, ROWS)
-        rad_up.append(
-            remote(
-                x_ref.at[:, shells - WIDTH : shells, part],
-                lo.at[:, :, part],
-                rad_send.at[0, c],
-                rad_recv.at[0, c],
-                (r + 1, a),
-            )
-        )
-        rad_down.append(
-            remote(
-                x_ref.at[:, 0:WIDTH, part],
-                hi.at[:, :, part],
-                rad_send.at[1, c],
-                rad_recv.at[1, c],
-                (r - 1, a),
-            )
-        )
+        above = x_ref.at[:, shells - WIDTH : shells, part]
+        below = x_ref.at[:, 0:WIDTH, part]
+        lo_part, hi_part = lo.at[:, :, part], hi.at[:, :, part]
+        up_sems = rad_send.at[0, c], rad_recv.at[0, c]
+        down_sems = rad_send.at[1, c], rad_recv.at[1, c]
+        rad_up.append(remote(above, lo_part, *up_sems, (r + 1, a)))
+        rad_down.append(remote(below, hi_part, *down_sems, (r - 1, a)))
+        if c < chunks - 1:
+            spot = relay.at[c]
+            far_up.append(remote(above, spot, up_sems[0], far_recv.at[c], (r + 2, a)))
+            far_down.append(remote(below, spot, down_sems[0], far_recv.at[c], (r - 2, a)))
+            pass_up.append(remote(spot, lo_part, pass_send.at[c], up_sems[1], (r - 1, a)))
+            pass_down.append(remote(spot, hi_part, pass_send.at[c], down_sems[1], (r + 1, a)))
+    odd = r % 2 == 1
+    even = r % 2 == 0
+    n_up_far = jnp.where(odd & (r + 2 < n_rad), (r + 1) // 2, 0)
+    n_down_far = jnp.where(even & (r > 0), chunks - r // 2, 0)
+    n_up_pass = jnp.where(odd & (r > 1), (r - 1) // 2, 0)
+    n_down_pass = jnp.where(even & (r + 2 < n_rad), chunks - 1 - r // 2, 0)
+
+    def start_far(c):
+        when(c < n_up_far, far_up[c].start)
+        when(c < n_down_far, far_down[c].start)
 
     def start_chunk(c):
-        when(r + 1 < n_rad, rad_up[c].start)
-        when(r > 0, rad_down[c].start)
+        when((r + 1 < n_rad) & (c >= n_up_far), rad_up[c].start)
+        when((r > 0) & (c >= n_down_far), rad_down[c].start)
+
+    def pass_on(c):
+        @pl.when(c < n_up_pass)
+        def _():
+            far_up[c].wait_recv()
+            pass_up[c].start()
+
+        @pl.when(c < n_down_pass)
+        def _():
+            far_down[c].wait_recv()
+            pass_down[c].start()
 
     when(a + 1 < n_ang, ang_up.start)
     when(a > 0, ang_down.start)
+    for c in range(chunks - 1):
+        start_far(c)
     start_chunk(0)
 
+    @pl.when(a == 0)
+    def _():
+        ext[:, :, 0:PADR, :] = jnp.zeros((4, shells, PADR, cols), f32)
+
+    @pl.when(a == n_ang - 1)
+    def _():
+        ext[:, :, PADR + rows : span, :] = jnp.zeros((4, shells, PADR, cols), f32)
+
+    @pl.when(r == 0)
+    def _():
+        lo[...] = jnp.zeros_like(lo)
+
+    @pl.when(r == n_rad - 1)
+    def _():
+        hi[...] = jnp.zeros_like(hi)
+
+    for d in range(1, n_rad):
+
+        @pl.when(r - d < 0)
+        def _():
+            got_up[d] = jnp.zeros((8, LANES), f32)
+
+        @pl.when(r + d >= n_rad)
+        def _():
+            got_down[d] = jnp.zeros((8, LANES), f32)
+
     load_rows.wait()
+    load_degree.wait()
     cosine = jnp.broadcast_to(rowtab[:, 0:1], (span, LANES))
     sine = jnp.broadcast_to(rowtab[:, 1:2], (span, LANES))
     order = lax.broadcasted_iota(jnp.int32, (span, LANES), 1) % MPAD
@@ -301,6 +336,8 @@
     lax.fori_loop(1, NK, next_level, (level, jnp.zeros_like(level)))
 
     load_density.wait()
+    load_high.wait()
+    load_low.wait()
     weight = sine[PADR : PADR + rows] * (step_t * step_p)
     half = shells // 2
     for h in range(2):
@@ -395,7 +432,8 @@
 
     exchange_b.wait_recv()
     total = mine[...] + got_b[...]
-    log_radius = log_ref[r]
+    load_log.wait()
+    log_radius = log_ref[...]
     shell = lax.broadcasted_iota(jnp.int32, (shells, LANES), 0)
     radius = inner_radius + step_r * ((r * shells + shell).astype(f32) + 0.5)
     order = lax.broadcasted_iota(jnp.int32, (shells, LANES), 1) % MPAD
@@ -425,7 +463,9 @@
     for d in range(1, n_rad):
         when(r + d < n_rad, exchange_up(d).start)
         when(r - d >= 0, exchange_down(d).start)
+    pass_on(0)
     start_chunk(2)
+    pass_on(1)
 
     lax.fori_loop(shells * tiles // 2, shells * tiles, theta_flux, 0)
 
@@ -455,6 +495,7 @@
 
     for d in range(1, GROUPS):
         exchange_d(d).start()
+    pass_on(2)
     start_chunk(3)
     for d in range(1, GROUPS):
         exchange_d(d).wait_recv()
@@ -488,6 +529,8 @@
             table[at + rows : at + 2 * rows, :] = slope
             table[at + 2 * rows : at + 3 * rows, :] = change * theta_scale
             table[at + 3 * rows : at + 4 * rows, :] = pltpu.roll(base, MPAD, 1) * slope_row
+
+    load_back.wait()
 
     def sources(i, carry):
         at = pl.multiple_of(i * 4 * rows, 4 * rows)
@@ -530,10 +573,7 @@
         return carry
 
     lax.fori_loop(0, shells, sources, 0)
-    store_pot = pltpu.make_async_copy(pot, pot_ref, out_sem.at[chunks])
-    store_pot.start()
-
-    stores = []
+
     for chunk in range(chunks):
         when(r > 0, rad_up[chunk].wait_recv)
         when(r + 1 < n_rad, rad_down[chunk].wait_recv)
@@ -577,17 +617,14 @@
             return carry
 
         lax.fori_loop(0, tiles, radial_flux, 0)
-        store = pltpu.make_async_copy(
-            tend.at[:, :, spot], inc_ref.at[:, :, spot], out_sem.at[chunk]
-        )
-        store.start()
-        stores.append(store)
 
     when(a + 1 < n_ang, ang_up.wait_send)
     when(a > 0, ang_down.wait_send)
     for c in range(chunks):
         when(r + 1 < n_rad, rad_up[c].wait_send)
         when(r > 0, rad_down[c].wait_send)
+        if c < chunks - 1:
+            when((c < n_up_pass) | (c < n_down_pass), pass_up[c].wait_send)
     for d in range(1, GROUPS):
         exchange_a(d).wait_send()
         exchange_d(d).wait_send()
@@ -595,9 +632,6 @@
     for d in range(1, n_rad):
         when(r + d < n_rad, exchange_up(d).wait_send)
         when(r - d >= 0, exchange_down(d).wait_send)
-    store_pot.wait()
-    for store in stores:
-        store.wait()
 
 
 def solution(mesh):
@@ -618,27 +652,30 @@
         )
         span = rows + 2 * PADR
         chunks = rows // ROWS
-        anywhere = pl.BlockSpec(memory_space=pl.ANY)
         inside = pl.BlockSpec(memory_space=pltpu.VMEM)
         dma = pltpu.SemaphoreType.DMA
         increment, potential = pl.pallas_call(
             functools.partial(kernel, n_rad, n_ang, shells, rows, cols),
             out_shape=(
-                jax.ShapeDtypeStruct(state.shape, f32),
-                jax.ShapeDtypeStruct(state.shape[1:], f32),
+                pltpu.VMEM(state.shape, f32),
+                pltpu.VMEM(state.shape[1:], f32),
             ),
-            in_specs=[anywhere, inside, inside, inside, anywhere, inside, inside],
-            out_specs=(anywhere, anywhere),
+            in_specs=[pl.BlockSpec(memory_space=pltpu.HBM)] * 7,
+            out_specs=(inside, inside),
             scratch_shapes=[
                 pltpu.VMEM((4, shells, span, cols), f32),
                 pltpu.VMEM((4, WIDTH, rows, cols), f32),
                 pltpu.VMEM((4, WIDTH, rows, cols), f32),
-                pltpu.VMEM((4, shells, rows, cols), f32),
-                pltpu.VMEM((shells, rows, cols), f32),
+                pltpu.VMEM((chunks - 1, 4, WIDTH, ROWS, cols), f32),
                 pltpu.VMEM((4 * rows, cols), f32),
                 pltpu.VMEM((shells * 4 * rows, LANES), f32),
                 pltpu.VMEM((shells * rows, LANES), f32),
+                pltpu.VMEM((cols, LANES), bf16),
+                pltpu.VMEM((cols, LANES), bf16),
+                pltpu.VMEM((3 * LANES, cols), bf16),
                 pltpu.VMEM((span, LANES), f32),
+                pltpu.VMEM((2 * NK + 8, LANES), f32),
+                pltpu.VMEM((shells, LANES), f32),
                 pltpu.VMEM((NK, span, LANES), f32),
                 pltpu.VMEM((GROUPS, KD, shells, LANES), f32),
                 pltpu.VMEM((GROUPS, KD, shells, LANES), f32),
@@ -649,12 +686,13 @@
                 pltpu.VMEM((n_rad, 8, LANES), f32),
                 pltpu.VMEM((n_rad, 8, LANES), f32),
                 pltpu.VMEM((GROUPS, 2, KD, shells, LANES), f32),
-                dma((3,)),
-                dma((chunks + 1,)),
+                dma((8,)),
                 dma((2,)),
                 dma((2,)),
                 dma((2, chunks)),
                 dma((2, chunks)),
+                dma((chunks - 1,)),
+                dma((chunks - 1,)),
                 dma((GROUPS,)),
                 dma((GROUPS,)),
                 dma((1,)),
@@ -665,7 +703,7 @@
                 dma((GROUPS,)),
             ],
             compiler_params=pltpu.CompilerParams(
-                collective_id=0, has_side_effects=True, vmem_limit_bytes=56 << 20
+                collective_id=0, has_side_effects=True, vmem_limit_bytes=61_700_000
             ),
         )(*operands)
         return increment, potential

time: 94.2 us -> 80.8 us (0.86)
  Pallas kernels: 87.6 us -> 77.1 us
  local copies, waits for them, and re-layouts: 5.85 us -> 2.99 us
    pallas_call x1, Pallas kernels: 87.6 us -> 77.1 us  [body(): pl.pallas_call(functools.partial(kernel, n_rad, n_ang, shells, rows, cols...]
    unnamed x4 -> x2, local copies, waits for them, and re-layouts: 5.85 us -> 2.99 us
where the time goes in v1:
time: 80.8 us; the launch traced here: 80.7 us
  Pallas kernels  77.1 us (95%)
  local copies, waits for them, and re-layouts  2.99 us (4%)
    pallas_call x1, Pallas kernels, body(): pl.pallas_call(functools.partial(kernel, n_rad, n_ang, shells, rows, cols...  77.1 us
    unnamed x2, local copies, waits for them, and re-layouts  2.99 us

profile of v1, /device:TPU:38, one launch (start us, length us, event | category | flops | bytes accessed | tf_op | source)
XLA Modules:
  0.0 80.7 jit_solution(1651320980346320612)
XLA Ops:
  0.6 77.1 %shard_map.86 = (f32[4,8,32,1024]{3,2,1,0:T(8,128)S(1)}, f32[8,32,1024]{2,1,0:T(8,128)S(1)}) custom-call(f32[4,8,32,1024]{3,2,1,0:T(8,128)} %x_ref.1, bf16[1024,128]{1,0:T(8,128)(2,1)} %constant.12.clone.fwd_high_hbm, bf16[1024,128]{1,0:T(8,128)(2,1)} %constant.13.clone.fwd_low_hbm, bf16[384,1024]{1,0:T(8,128)(2,1)} %constant.14.clone.back_hbm, ...), custom_call_target="tpu_custom_call" | custom-call | tf_op jit(solution)/shard_map/pallas_call | solution.py:657
  77.7 2.0 %copy.11 = f32[4,8,32,1024]{3,2,1,0:T(8,128)} copy(f32[4,8,32,1024]{3,2,1,0:T(8,128)S(1)} %get-tuple-element.2) | data formatting | bytes 8388608
  79.7 1.0 %copy.12 = f32[8,32,1024]{2,1,0:T(8,128)} copy(f32[8,32,1024]{2,1,0:T(8,128)S(1)} %get-tuple-element.3) | data formatting | bytes 2097152

commit v2 on v1

--- a/solution.py
+++ b/solution.py
@@ -18,6 +18,7 @@
 PADR = 8
 WIDTH = 3
 ROWS = 8
+CUTS = 2
 
 sound_speed = 0.5
 sound_sq = 0.25
@@ -137,10 +138,10 @@
     got_a,
     mine,
     got_b,
-    tot_up,
-    tot_down,
-    got_up,
-    got_down,
+    totals,
+    got_pair,
+    chain_up,
+    chain_down,
     coef,
     local_sem,
     ang_send,
@@ -163,6 +164,9 @@
     y, x_hi, core = a // 4, (a // 2) % 2, a % 2
     g = y * 2 + core
     chunks = rows // ROWS
+    parts = chunks * CUTS
+    wide = cols // CUTS
+    n_far = parts - CUTS
     span = rows + 2 * PADR
     own = pl.ds(PADR, rows)
     step_r = radial_span / (n_rad * shells)
@@ -208,21 +212,22 @@
             lambda: pl.semaphore_signal(barrier, inc=1, device_id=dev, device_id_type=MESH),
         )
 
-    for d in range(1, n_rad):
+    ends = jnp.where(a > 0, 1, 0) + jnp.where(a + 1 < n_ang, 1, 0)
+    for d in (1, 2):
         greet(r + d < n_rad, (r + d, a))
         greet(r - d >= 0, (r - d, a))
+        ends = ends + jnp.where(r + d < n_rad, 1, 0) + jnp.where(r - d >= 0, 1, 0)
     for d in range(1, GROUPS):
         pl.semaphore_signal(barrier, inc=1, device_id=peer(d), device_id_type=MESH)
     pl.semaphore_signal(barrier, inc=1, device_id=partner, device_id_type=MESH)
     greet(a + 1 < n_ang, (r, a + 1))
     greet(a > 0, (r, a - 1))
-    ends = jnp.where(a > 0, 1, 0) + jnp.where(a + 1 < n_ang, 1, 0)
 
     for load in (load_rows, load_degree, load_density, load_high, load_low):
         load.start()
     for load in (load_rest, load_log, load_back):
         load.start()
-    pl.semaphore_wait(barrier, n_rad - 1 + GROUPS + ends)
+    pl.semaphore_wait(barrier, GROUPS + ends)
 
     ang_up = remote(
         x_ref.at[:, :, rows - WIDTH : rows],
@@ -239,16 +244,17 @@
         (r, a - 1),
     )
     rad_up, rad_down, far_up, far_down, pass_up, pass_down = [], [], [], [], [], []
-    for c in range(chunks):
-        part = pl.ds(c * ROWS, ROWS)
-        above = x_ref.at[:, shells - WIDTH : shells, part]
-        below = x_ref.at[:, 0:WIDTH, part]
-        lo_part, hi_part = lo.at[:, :, part], hi.at[:, :, part]
+    for c in range(parts):
+        part = pl.ds((c // CUTS) * ROWS, ROWS)
+        band = pl.ds((c % CUTS) * wide, wide)
+        above = x_ref.at[:, shells - WIDTH : shells, part, band]
+        below = x_ref.at[:, 0:WIDTH, part, band]
+        lo_part, hi_part = lo.at[:, :, part, band], hi.at[:, :, part, band]
         up_sems = rad_send.at[0, c], rad_recv.at[0, c]
         down_sems = rad_send.at[1, c], rad_recv.at[1, c]
         rad_up.append(remote(above, lo_part, *up_sems, (r + 1, a)))
         rad_down.append(remote(below, hi_part, *down_sems, (r - 1, a)))
-        if c < chunks - 1:
+        if c < n_far:
             spot = relay.at[c]
             far_up.append(remote(above, spot, up_sems[0], far_recv.at[c], (r + 2, a)))
             far_down.append(remote(below, spot, down_sems[0], far_recv.at[c], (r - 2, a)))
@@ -256,10 +262,10 @@
             pass_down.append(remote(spot, hi_part, pass_send.at[c], down_sems[1], (r + 1, a)))
     odd = r % 2 == 1
     even = r % 2 == 0
-    n_up_far = jnp.where(odd & (r + 2 < n_rad), (r + 1) // 2, 0)
-    n_down_far = jnp.where(even & (r > 0), chunks - r // 2, 0)
-    n_up_pass = jnp.where(odd & (r > 1), (r - 1) // 2, 0)
-    n_down_pass = jnp.where(even & (r + 2 < n_rad), chunks - 1 - r // 2, 0)
+    n_up_far = jnp.where(odd & (r + 2 < n_rad), CUTS * ((r + 1) // 2), 0)
+    n_down_far = jnp.where(even & (r > 0), parts - CUTS * (r // 2), 0)
+    n_up_pass = jnp.where(odd & (r > 1), CUTS * ((r - 1) // 2), 0)
+    n_down_pass = jnp.where(even & (r + 2 < n_rad), n_far - CUTS * (r // 2), 0)
 
     def start_far(c):
         when(c < n_up_far, far_up[c].start)
@@ -282,9 +288,10 @@
 
     when(a + 1 < n_ang, ang_up.start)
     when(a > 0, ang_down.start)
-    for c in range(chunks - 1):
+    for c in range(n_far):
         start_far(c)
-    start_chunk(0)
+    for c in range(CUTS):
+        start_chunk(c)
 
     @pl.when(a == 0)
     def _():
@@ -302,15 +309,13 @@
     def _():
         hi[...] = jnp.zeros_like(hi)
 
-    for d in range(1, n_rad):
-
-        @pl.when(r - d < 0)
-        def _():
-            got_up[d] = jnp.zeros((8, LANES), f32)
-
-        @pl.when(r + d >= n_rad)
-        def _():
-            got_down[d] = jnp.zeros((8, LANES), f32)
+    @pl.when(r < 2)
+    def _():
+        chain_up[1:] = jnp.zeros((n_rad // 2 - 1, 8, LANES), f32)
+
+    @pl.when(r + 2 >= n_rad)
+    def _():
+        chain_down[1:] = jnp.zeros((n_rad // 2 - 1, 8, LANES), f32)
 
     load_rows.wait()
     load_degree.wait()
@@ -400,7 +405,8 @@
     mine[...] = total
     exchange_b = remote(mine, got_b, b_send.at[0], b_recv.at[0], partner)
     exchange_b.start()
-    start_chunk(1)
+    for c in range(CUTS, 2 * CUTS):
+        start_chunk(c)
 
     lax.fori_loop(shells * chunks // 2, shells * chunks, phi_flux, 0)
 
@@ -428,7 +434,7 @@
             tend[c, i, :, lanes] = tend[c, i, :, lanes] + change[PADR : PADR + rows]
         return carry
 
-    lax.fori_loop(0, shells * tiles // 2, theta_flux, 0)
+    lax.fori_loop(0, shells * tiles // 4, theta_flux, 0)
 
     exchange_b.wait_recv()
     total = mine[...] + got_b[...]
@@ -447,36 +453,60 @@
         for s in (1, 2, 4):
             up = up + jnp.where(shell >= s, pltpu.roll(up, s, 0), 0.0)
             down = down + jnp.where(shell >= s, pltpu.roll(down, s, 0), 0.0)
-        tot_up[q : q + 1, :] = up[shells - 1 : shells]
-        tot_down[q : q + 1, :] = down[shells - 1 : shells]
+        totals[0, q : q + 1, :] = up[shells - 1 : shells]
+        totals[1, q : q + 1, :] = down[shells - 1 : shells]
         ups.append(up)
         downs.append(down)
         powers.append(grow)
         degrees.append(degree)
 
-    def exchange_up(d):
-        return remote(tot_up, got_up.at[d], c_send.at[0, d], c_recv.at[0, d], (r + d, a))
-
-    def exchange_down(d):
-        return remote(tot_down, got_down.at[d], c_send.at[1, d], c_recv.at[1, d], (r - d, a))
-
-    for d in range(1, n_rad):
-        when(r + d < n_rad, exchange_up(d).start)
-        when(r - d >= 0, exchange_down(d).start)
-    pass_on(0)
-    start_chunk(2)
-    pass_on(1)
-
-    lax.fori_loop(shells * tiles // 2, shells * tiles, theta_flux, 0)
-
-    for d in range(1, n_rad):
-        when(r - d >= 0, exchange_up(d).wait_recv)
-        when(r + d < n_rad, exchange_down(d).wait_recv)
-    below = got_up[1]
-    above = got_down[1]
-    for d in range(2, n_rad):
-        below = below + got_up[d]
-        above = above + got_down[d]
+    pair = remote(totals, got_pair, c_send.at[0, 0], c_recv.at[0, 0], (r + 1 - 2 * (r % 2), a))
+    pair.start()
+
+    def hop_up(d):
+        return remote(
+            chain_up.at[d - 1], chain_up.at[d], c_send.at[0, d], c_recv.at[0, d], (r + 2, a)
+        )
+
+    def hop_down(d):
+        return remote(
+            chain_down.at[d - 1], chain_down.at[d], c_send.at[1, d], c_recv.at[1, d], (r - 2, a)
+        )
+
+    def start_hop(d):
+        when(r + 2 < n_rad, hop_up(d).start)
+        when(r - 2 >= 0, hop_down(d).start)
+
+    def end_hop(d):
+        when(r - 2 >= 0, hop_up(d).wait_recv)
+        when(r + 2 < n_rad, hop_down(d).wait_recv)
+
+    for c in range(2 * CUTS, 3 * CUTS):
+        pass_on(c - 2 * CUTS)
+        start_chunk(c)
+    for c in range(CUTS, 2 * CUTS):
+        pass_on(c)
+
+    quarter = shells * tiles // 4
+    lax.fori_loop(quarter, 2 * quarter, theta_flux, 0)
+    pair.wait_recv()
+    pair_up = got_pair[0]
+    pair_down = got_pair[1]
+    chain_up[0] = totals[0] + pair_up
+    chain_down[0] = totals[1] + pair_down
+    start_hop(1)
+    lax.fori_loop(2 * quarter, 3 * quarter, theta_flux, 0)
+    end_hop(1)
+    start_hop(2)
+    lax.fori_loop(3 * quarter, 4 * quarter, theta_flux, 0)
+    end_hop(2)
+    start_hop(3)
+    below = jnp.where(odd, pair_up, 0.0)
+    above = jnp.where(even, pair_down, 0.0)
+    end_hop(3)
+    for d in range(1, n_rad // 2):
+        below = below + chain_up[d]
+        above = above + chain_down[d]
     inverse_radius = 1.0 / radius
     for q in range(KD):
         inner = below[q : q + 1] + ups[q]
@@ -495,8 +525,9 @@
 
     for d in range(1, GROUPS):
         exchange_d(d).start()
-    pass_on(2)
-    start_chunk(3)
+    for c in range(2 * CUTS, 3 * CUTS):
+        pass_on(c)
+        start_chunk(c + CUTS)
     for d in range(1, GROUPS):
         exchange_d(d).wait_recv()
 
@@ -574,11 +605,13 @@
 
     lax.fori_loop(0, shells, sources, 0)
 
-    for chunk in range(chunks):
+    per = wide // LANES
+    for chunk in range(parts):
         when(r > 0, rad_up[chunk].wait_recv)
         when(r + 1 < n_rad, rad_down[chunk].wait_recv)
-        at = chunk * ROWS
+        at = (chunk // CUTS) * ROWS
         spot = pl.ds(at, ROWS)
+        first = (chunk % CUTS) * per
 
         def radial_flux(tile, carry):
             lanes = pl.ds(pl.multiple_of(tile * LANES, LANES), LANES)
@@ -616,22 +649,34 @@
                 last = face
             return carry
 
-        lax.fori_loop(0, tiles, radial_flux, 0)
+        lax.fori_loop(first, first + per, radial_flux, 0)
 
     when(a + 1 < n_ang, ang_up.wait_send)
     when(a > 0, ang_down.wait_send)
-    for c in range(chunks):
+    for c in range(parts):
         when(r + 1 < n_rad, rad_up[c].wait_send)
         when(r > 0, rad_down[c].wait_send)
-        if c < chunks - 1:
+        if c < n_far:
             when((c < n_up_pass) | (c < n_down_pass), pass_up[c].wait_send)
     for d in range(1, GROUPS):
         exchange_a(d).wait_send()
         exchange_d(d).wait_send()
     exchange_b.wait_send()
-    for d in range(1, n_rad):
-        when(r + d < n_rad, exchange_up(d).wait_send)
-        when(r - d >= 0, exchange_down(d).wait_send)
+    pair.wait_send()
+    for d in range(1, n_rad // 2):
+        when(r + 2 < n_rad, hop_up(d).wait_send)
+        when(r - 2 >= 0, hop_down(d).wait_send)
+
+
+def store(tend, pot, inc_ref, pot_ref, sem):
+    copies = [
+        pltpu.make_async_copy(tend.at[c], inc_ref.at[c], sem.at[c]) for c in range(tend.shape[0])
+    ]
+    copies.append(pltpu.make_async_copy(pot, pot_ref, sem.at[len(copies)]))
+    for copy in copies:
+        copy.start()
+    for copy in copies:
+        copy.wait()
 
 
 def solution(mesh):
@@ -651,7 +696,7 @@
             jnp.asarray(log_radii(n_rad, shells)),
         )
         span = rows + 2 * PADR
-        chunks = rows // ROWS
+        parts = (rows // ROWS) * CUTS
         inside = pl.BlockSpec(memory_space=pltpu.VMEM)
         dma = pltpu.SemaphoreType.DMA
         increment, potential = pl.pallas_call(
@@ -666,7 +711,7 @@
                 pltpu.VMEM((4, shells, span, cols), f32),
                 pltpu.VMEM((4, WIDTH, rows, cols), f32),
                 pltpu.VMEM((4, WIDTH, rows, cols), f32),
-                pltpu.VMEM((chunks - 1, 4, WIDTH, ROWS, cols), f32),
+                pltpu.VMEM((parts - CUTS, 4, WIDTH, ROWS, cols // CUTS), f32),
                 pltpu.VMEM((4 * rows, cols), f32),
                 pltpu.VMEM((shells * 4 * rows, LANES), f32),
                 pltpu.VMEM((shells * rows, LANES), f32),
@@ -681,24 +726,24 @@
                 pltpu.VMEM((GROUPS, KD, shells, LANES), f32),
                 pltpu.VMEM((KD, shells, LANES), f32),
                 pltpu.VMEM((KD, shells, LANES), f32),
-                pltpu.VMEM((8, LANES), f32),
-                pltpu.VMEM((8, LANES), f32),
-                pltpu.VMEM((n_rad, 8, LANES), f32),
-                pltpu.VMEM((n_rad, 8, LANES), f32),
+                pltpu.VMEM((2, 8, LANES), f32),
+                pltpu.VMEM((2, 8, LANES), f32),
+                pltpu.VMEM((n_rad // 2, 8, LANES), f32),
+                pltpu.VMEM((n_rad // 2, 8, LANES), f32),
                 pltpu.VMEM((GROUPS, 2, KD, shells, LANES), f32),
                 dma((8,)),
                 dma((2,)),
                 dma((2,)),
-                dma((2, chunks)),
-                dma((2, chunks)),
-                dma((chunks - 1,)),
-                dma((chunks - 1,)),
+                dma((2, parts)),
+                dma((2, parts)),
+                dma((parts - CUTS,)),
+                dma((parts - CUTS,)),
                 dma((GROUPS,)),
                 dma((GROUPS,)),
                 dma((1,)),
                 dma((1,)),
-                dma((2, n_rad)),
-                dma((2, n_rad)),
+                dma((2, n_rad // 2)),
+                dma((2, n_rad // 2)),
                 dma((GROUPS,)),
                 dma((GROUPS,)),
             ],
@@ -706,7 +751,18 @@
                 collective_id=0, has_side_effects=True, vmem_limit_bytes=61_700_000
             ),
         )(*operands)
-        return increment, potential
+        outside = pl.BlockSpec(memory_space=pltpu.HBM)
+        return pl.pallas_call(
+            store,
+            out_shape=(
+                jax.ShapeDtypeStruct(state.shape, f32),
+                jax.ShapeDtypeStruct(state.shape[1:], f32),
+            ),
+            in_specs=(inside, inside),
+            out_specs=(outside, outside),
+            scratch_shapes=[dma((5,))],
+            compiler_params=pltpu.CompilerParams(vmem_limit_bytes=1 << 20),
+        )(increment, potential)
 
     return jax.shard_map(
         body,

time: 80.8 us -> 79.6 us (0.985)
  local copies, waits for them, and re-layouts: 2.99 us -> 0 us
  Pallas kernels: 77.1 us -> 78.8 us
    unnamed x2 -> x0, local copies, waits for them, and re-layouts: 2.99 us -> none
    pallas_call x0 -> x1, Pallas kernels: none -> 2.4 us  [body(): pl.pallas_call(store, out_shape=(jax.ShapeDtypeStruct(state.shape, f32),...]
where the time goes in v2:
time: 79.6 us; the launch traced here: 79.5 us
  Pallas kernels  78.8 us (99%)
    pallas_call x1, Pallas kernels, body(): pl.pallas_call(functools.partial(kernel, n_rad, n_ang, shells, rows, cols...  76.4 us
    pallas_call x1, Pallas kernels, body(): pl.pallas_call(store, out_shape=(jax.ShapeDtypeStruct(state.shape, f32),...  2.4 us

profile of v2, /device:TPU:38, one launch (start us, length us, event | category | flops | bytes accessed | tf_op | source)
XLA Modules:
  0.0 79.5 jit_solution(6519993771330210424)
XLA Ops:
  0.6 76.4 %shard_map.86 = (f32[4,8,32,1024]{3,2,1,0:T(8,128)S(1)}, f32[8,32,1024]{2,1,0:T(8,128)S(1)}) custom-call(f32[4,8,32,1024]{3,2,1,0:T(8,128)} %x_ref.1, bf16[1024,128]{1,0:T(8,128)(2,1)} %constant.12.clone.fwd_high_hbm, bf16[1024,128]{1,0:T(8,128)(2,1)} %constant.13.clone.fwd_low_hbm, bf16[384,1024]{1,0:T(8,128)(2,1)} %constant.14.clone.back_hbm, ...), custom_call_target="tpu_custom_call" | custom-call | tf_op jit(solution)/shard_map/pallas_call | solution.py:702
  77.1 2.4 %shard_map.87 = (f32[4,8,32,1024]{3,2,1,0:T(8,128)}, f32[8,32,1024]{2,1,0:T(8,128)}) custom-call(f32[4,8,32,1024]{3,2,1,0:T(8,128)S(1)} %get-tuple-element.4.tend, f32[8,32,1024]{2,1,0:T(8,128)S(1)} %get-tuple-element.5.pot), custom_call_target="tpu_custom_call" | custom-call | tf_op jit(solution)/shard_map/pallas_call | solution.py:755

commit v3 on v2

--- a/solution.py
+++ b/solution.py
@@ -18,6 +18,7 @@
 PADR = 8
 WIDTH = 3
 ROWS = 8
+QUARTERS = 4
 CUTS = 2
 
 sound_speed = 0.5
@@ -124,6 +125,7 @@
     lo,
     hi,
     relay,
+    row_relay,
     fields,
     table,
     spec,
@@ -146,6 +148,8 @@
     local_sem,
     ang_send,
     ang_recv,
+    skip_recv,
+    hand_send,
     rad_send,
     rad_recv,
     far_recv,
@@ -212,37 +216,69 @@
             lambda: pl.semaphore_signal(barrier, inc=1, device_id=dev, device_id_type=MESH),
         )
 
+    first = a % 4 == 0
+    last = a % 4 == 3
+    greet(a + 1 < n_ang, (r, a + 1))
+    greet(a > 0, (r, a - 1))
+    greet(first, (r, a + 3))
+    greet(last, (r, a - 3))
     ends = jnp.where(a > 0, 1, 0) + jnp.where(a + 1 < n_ang, 1, 0)
+    ends = ends + jnp.where(first | last, 1, 0)
     for d in (1, 2):
         greet(r + d < n_rad, (r + d, a))
         greet(r - d >= 0, (r - d, a))
         ends = ends + jnp.where(r + d < n_rad, 1, 0) + jnp.where(r - d >= 0, 1, 0)
+    pl.semaphore_signal(barrier, inc=1, device_id=partner, device_id_type=MESH)
     for d in range(1, GROUPS):
         pl.semaphore_signal(barrier, inc=1, device_id=peer(d), device_id_type=MESH)
-    pl.semaphore_signal(barrier, inc=1, device_id=partner, device_id_type=MESH)
-    greet(a + 1 < n_ang, (r, a + 1))
-    greet(a > 0, (r, a - 1))
-
     for load in (load_rows, load_degree, load_density, load_high, load_low):
         load.start()
     for load in (load_rest, load_log, load_back):
         load.start()
     pl.semaphore_wait(barrier, GROUPS + ends)
 
-    ang_up = remote(
-        x_ref.at[:, :, rows - WIDTH : rows],
-        ext.at[:, :, PADR - WIDTH : PADR],
-        ang_send.at[0],
-        ang_recv.at[0],
-        (r, a + 1),
-    )
-    ang_down = remote(
-        x_ref.at[:, :, 0:WIDTH],
-        ext.at[:, :, PADR + rows : PADR + rows + WIDTH],
-        ang_send.at[1],
-        ang_recv.at[1],
-        (r, a - 1),
-    )
+    deep = shells // QUARTERS
+    rows_up, rows_down, skip_up, skip_down, hand_up, hand_down = [], [], [], [], [], []
+    for c in range(QUARTERS):
+        part = pl.ds(c * deep, deep)
+        high = x_ref.at[:, part, rows - WIDTH : rows]
+        low = x_ref.at[:, part, 0:WIDTH]
+        under = ext.at[:, part, PADR - WIDTH : PADR]
+        over = ext.at[:, part, PADR + rows : PADR + rows + WIDTH]
+        up_sems = ang_send.at[0, c], ang_recv.at[0, c]
+        down_sems = ang_send.at[1, c], ang_recv.at[1, c]
+        rows_up.append(remote(high, under, *up_sems, (r, a + 1)))
+        rows_down.append(remote(low, over, *down_sems, (r, a - 1)))
+        if c < QUARTERS - 1:
+            spot = row_relay.at[c]
+            skip_up.append(remote(high, spot, up_sems[0], skip_recv.at[c], (r, a + 4)))
+            skip_down.append(remote(low, spot, down_sems[0], skip_recv.at[c], (r, a - 4)))
+            hand_up.append(remote(spot, under, hand_send.at[c], up_sems[1], (r, a - 3)))
+            hand_down.append(remote(spot, over, hand_send.at[c], down_sems[1], (r, a + 3)))
+    n_up_skip = jnp.where(last & (a + 1 < n_ang), y + 1, 0)
+    n_down_skip = jnp.where(first & (a > 0), QUARTERS - y, 0)
+    n_up_hand = jnp.where(last, y, 0)
+    n_down_hand = jnp.where(first, QUARTERS - 1 - y, 0)
+
+    def start_rows(c):
+        when((a + 1 < n_ang) & (c >= n_up_skip), rows_up[c].start)
+        when((a > 0) & (c >= n_down_skip), rows_down[c].start)
+
+    def start_skip(c):
+        when(c < n_up_skip, skip_up[c].start)
+        when(c < n_down_skip, skip_down[c].start)
+
+    def hand_on(c):
+        @pl.when(c < n_up_hand)
+        def _():
+            skip_up[c].wait_recv()
+            hand_up[c].start()
+
+        @pl.when(c < n_down_hand)
+        def _():
+            skip_down[c].wait_recv()
+            hand_down[c].start()
+
     rad_up, rad_down, far_up, far_down, pass_up, pass_down = [], [], [], [], [], []
     for c in range(parts):
         part = pl.ds((c // CUTS) * ROWS, ROWS)
@@ -286,8 +322,10 @@
             far_down[c].wait_recv()
             pass_down[c].start()
 
-    when(a + 1 < n_ang, ang_up.start)
-    when(a > 0, ang_down.start)
+    for c in range(QUARTERS - 1):
+        start_skip(c)
+    for c in range(QUARTERS):
+        start_rows(c)
     for c in range(n_far):
         start_far(c)
     for c in range(CUTS):
@@ -339,6 +377,9 @@
         return (new, last)
 
     lax.fori_loop(1, NK, next_level, (level, jnp.zeros_like(level)))
+
+    for c in range(QUARTERS - 1):
+        hand_on(c)
 
     load_density.wait()
     load_high.wait()
@@ -410,8 +451,9 @@
 
     lax.fori_loop(shells * chunks // 2, shells * chunks, phi_flux, 0)
 
-    when(a > 0, ang_up.wait_recv)
-    when(a + 1 < n_ang, ang_down.wait_recv)
+    for c in range(QUARTERS):
+        when(a > 0, rows_up[c].wait_recv)
+        when(a + 1 < n_ang, rows_down[c].wait_recv)
     tiles = cols // LANES
 
     def theta_flux(index, carry):
@@ -651,8 +693,11 @@
 
         lax.fori_loop(first, first + per, radial_flux, 0)
 
-    when(a + 1 < n_ang, ang_up.wait_send)
-    when(a > 0, ang_down.wait_send)
+    for c in range(QUARTERS):
+        when(a + 1 < n_ang, rows_up[c].wait_send)
+        when(a > 0, rows_down[c].wait_send)
+        if c < QUARTERS - 1:
+            when((c < n_up_hand) | (c < n_down_hand), hand_up[c].wait_send)
     for c in range(parts):
         when(r + 1 < n_rad, rad_up[c].wait_send)
         when(r > 0, rad_down[c].wait_send)
@@ -712,6 +757,7 @@
                 pltpu.VMEM((4, WIDTH, rows, cols), f32),
                 pltpu.VMEM((4, WIDTH, rows, cols), f32),
                 pltpu.VMEM((parts - CUTS, 4, WIDTH, ROWS, cols // CUTS), f32),
+                pltpu.VMEM((QUARTERS - 1, 4, shells // QUARTERS, WIDTH, cols), f32),
                 pltpu.VMEM((4 * rows, cols), f32),
                 pltpu.VMEM((shells * 4 * rows, LANES), f32),
                 pltpu.VMEM((shells * rows, LANES), f32),
@@ -732,8 +778,10 @@
                 pltpu.VMEM((n_rad // 2, 8, LANES), f32),
                 pltpu.VMEM((GROUPS, 2, KD, shells, LANES), f32),
                 dma((8,)),
-                dma((2,)),
-                dma((2,)),
+                dma((2, QUARTERS)),
+                dma((2, QUARTERS)),
+                dma((QUARTERS - 1,)),
+                dma((QUARTERS - 1,)),
                 dma((2, parts)),
                 dma((2, parts)),
                 dma((parts - CUTS,)),

time: 79.6 us -> 78.9 us (level)
  Pallas kernels: 78.8 us -> 78 us
    pallas_call x1, Pallas kernels: 76.4 us -> 75.6 us  [body(): pl.pallas_call(functools.partial(kernel, n_rad, n_ang, shells, rows, cols...]
where the time goes in v3:
time: 78.9 us; the launch traced here: 78.6 us
  Pallas kernels  78 us (99%)
    pallas_call x1, Pallas kernels, body(): pl.pallas_call(functools.partial(kernel, n_rad, n_ang, shells, rows, cols...  75.6 us
    pallas_call x1, Pallas kernels, body(): pl.pallas_call(store, out_shape=(jax.ShapeDtypeStruct(state.shape, f32),...  2.4 us

profile of v3, /device:TPU:38, one launch (start us, length us, event | category | flops | bytes accessed | tf_op | source)
XLA Modules:
  0.0 78.6 jit_solution(10148710297439587270)
XLA Ops:
  0.6 75.6 %shard_map.86 = (f32[4,8,32,1024]{3,2,1,0:T(8,128)S(1)}, f32[8,32,1024]{2,1,0:T(8,128)S(1)}) custom-call(f32[4,8,32,1024]{3,2,1,0:T(8,128)} %x_ref.1, bf16[1024,128]{1,0:T(8,128)(2,1)} %constant.12.clone.fwd_high_hbm, bf16[1024,128]{1,0:T(8,128)(2,1)} %constant.13.clone.fwd_low_hbm, bf16[384,1024]{1,0:T(8,128)(2,1)} %constant.14.clone.back_hbm, ...), custom_call_target="tpu_custom_call" | custom-call | tf_op jit(solution)/shard_map/pallas_call | solution.py:747
  76.2 2.4 %shard_map.87 = (f32[4,8,32,1024]{3,2,1,0:T(8,128)}, f32[8,32,1024]{2,1,0:T(8,128)}) custom-call(f32[4,8,32,1024]{3,2,1,0:T(8,128)S(1)} %get-tuple-element.4.tend, f32[8,32,1024]{2,1,0:T(8,128)S(1)} %get-tuple-element.5.pot), custom_call_target="tpu_custom_call" | custom-call | tf_op jit(solution)/shard_map/pallas_call | solution.py:803

commit v4 on v3

--- a/solution.py
+++ b/solution.py
@@ -145,6 +145,7 @@
     chain_up,
     chain_down,
     coef,
+    rounds,
     local_sem,
     ang_send,
     ang_recv,
@@ -209,33 +210,47 @@
     load_log = pltpu.make_async_copy(log_hbm.at[r], log_ref, local_sem.at[6])
     load_back = pltpu.make_async_copy(back_hbm, back_ref, local_sem.at[7])
     barrier = pltpu.get_barrier_semaphore()
-
-    def greet(cond, dev):
-        when(
-            cond,
-            lambda: pl.semaphore_signal(barrier, inc=1, device_id=dev, device_id_type=MESH),
-        )
-
     first = a % 4 == 0
     last = a % 4 == 3
-    greet(a + 1 < n_ang, (r, a + 1))
-    greet(a > 0, (r, a - 1))
-    greet(first, (r, a + 3))
-    greet(last, (r, a - 3))
-    ends = jnp.where(a > 0, 1, 0) + jnp.where(a + 1 < n_ang, 1, 0)
-    ends = ends + jnp.where(first | last, 1, 0)
-    for d in (1, 2):
-        greet(r + d < n_rad, (r + d, a))
-        greet(r - d >= 0, (r - d, a))
-        ends = ends + jnp.where(r + d < n_rad, 1, 0) + jnp.where(r - d >= 0, 1, 0)
-    pl.semaphore_signal(barrier, inc=1, device_id=partner, device_id_type=MESH)
-    for d in range(1, GROUPS):
-        pl.semaphore_signal(barrier, inc=1, device_id=peer(d), device_id_type=MESH)
+    odd = r % 2 == 1
+    even = r % 2 == 0
+    x = x_hi * 2 + r % 2
+
+    def along_x(step):
+        to = (x + step) % 4
+        return ((r // 2) * 2 + to % 2, y * 4 + (to // 2) * 2 + core)
+
+    near = [
+        (None, along_x(1)),
+        (None, along_x(3)),
+        (r + 2 < n_rad, (r + 2, a)),
+        (r - 2 >= 0, (r - 2, a)),
+        (a + 4 < n_ang, (r, a + 4)),
+        (a - 4 >= 0, (r, a - 4)),
+        (None, (r, a + 1 - 2 * core)),
+    ]
+    n_near = 3
+    for cond, _ in near:
+        if cond is not None:
+            n_near = n_near + jnp.where(cond, 1, 0)
+
+    def greet(sem):
+        for cond, dev in near:
+            signal = functools.partial(
+                pl.semaphore_signal, sem, inc=1, device_id=dev, device_id_type=MESH
+            )
+            if cond is None:
+                signal()
+            else:
+                when(cond, signal)
+
+    greet(barrier)
     for load in (load_rows, load_degree, load_density, load_high, load_low):
         load.start()
     for load in (load_rest, load_log, load_back):
         load.start()
-    pl.semaphore_wait(barrier, GROUPS + ends)
+    pl.semaphore_wait(barrier, n_near)
+    greet(rounds.at[0])
 
     deep = shells // QUARTERS
     rows_up, rows_down, skip_up, skip_down, hand_up, hand_down = [], [], [], [], [], []
@@ -296,8 +311,6 @@
             far_down.append(remote(below, spot, down_sems[0], far_recv.at[c], (r - 2, a)))
             pass_up.append(remote(spot, lo_part, pass_send.at[c], up_sems[1], (r - 1, a)))
             pass_down.append(remote(spot, hi_part, pass_send.at[c], down_sems[1], (r + 1, a)))
-    odd = r % 2 == 1
-    even = r % 2 == 0
     n_up_far = jnp.where(odd & (r + 2 < n_rad), CUTS * ((r + 1) // 2), 0)
     n_down_far = jnp.where(even & (r > 0), parts - CUTS * (r // 2), 0)
     n_up_pass = jnp.where(odd & (r > 1), CUTS * ((r - 1) // 2), 0)
@@ -307,9 +320,17 @@
         when(c < n_up_far, far_up[c].start)
         when(c < n_down_far, far_down[c].start)
 
+    def start_pair(c):
+        when(even, rad_up[c].start)
+        when(odd, rad_down[c].start)
+
+    def start_diagonal(c):
+        when(odd & (r + 1 < n_rad) & (c >= n_up_far), rad_up[c].start)
+        when(even & (r > 0) & (c >= n_down_far), rad_down[c].start)
+
     def start_chunk(c):
-        when((r + 1 < n_rad) & (c >= n_up_far), rad_up[c].start)
-        when((r > 0) & (c >= n_down_far), rad_down[c].start)
+        start_pair(c)
+        start_diagonal(c)
 
     def pass_on(c):
         @pl.when(c < n_up_pass)
@@ -322,14 +343,22 @@
             far_down[c].wait_recv()
             pass_down[c].start()
 
+    start_pair(0)
+    for c in range(n_far):
+        start_far(c)
     for c in range(QUARTERS - 1):
         start_skip(c)
+    for c in range(1, CUTS):
+        start_pair(c)
+    pl.semaphore_wait(rounds.at[0], n_near)
+    greet(rounds.at[1])
+    for c in range(CUTS):
+        start_diagonal(c)
+    pl.semaphore_wait(rounds.at[1], n_near)
+    greet(rounds.at[2])
+    pl.semaphore_wait(rounds.at[2], n_near)
     for c in range(QUARTERS):
         start_rows(c)
-    for c in range(n_far):
-        start_far(c)
-    for c in range(CUTS):
-        start_chunk(c)
 
     @pl.when(a == 0)
     def _():
@@ -777,6 +806,7 @@
                 pltpu.VMEM((n_rad // 2, 8, LANES), f32),
                 pltpu.VMEM((n_rad // 2, 8, LANES), f32),
                 pltpu.VMEM((GROUPS, 2, KD, shells, LANES), f32),
+                pltpu.SemaphoreType.REGULAR((3,)),
                 dma((8,)),
                 dma((2, QUARTERS)),
                 dma((2, QUARTERS)),

time: 78.9 us -> 77.5 us (0.982); the launches traced: 78.6 us -> 76.4 us
  Pallas kernels: 78 us -> 75.8 us
    pallas_call x1, Pallas kernels: 75.6 us -> 73.4 us  [body(): pl.pallas_call(functools.partial(kernel, n_rad, n_ang, shells, rows, cols...]
where the time goes in v4:
time: 77.5 us; the launch traced here: 76.4 us
  Pallas kernels  75.8 us (98%)
    pallas_call x1, Pallas kernels, body(): pl.pallas_call(functools.partial(kernel, n_rad, n_ang, shells, rows, cols...  73.4 us
    pallas_call x1, Pallas kernels, body(): pl.pallas_call(store, out_shape=(jax.ShapeDtypeStruct(state.shape, f32),...  2.4 us

profile of v4, /device:TPU:38, one launch (start us, length us, event | category | flops | bytes accessed | tf_op | source)
XLA Modules:
  0.0 76.4 jit_solution(16704156046611265408)
XLA Ops:
  0.6 73.4 %shard_map.86 = (f32[4,8,32,1024]{3,2,1,0:T(8,128)S(1)}, f32[8,32,1024]{2,1,0:T(8,128)S(1)}) custom-call(f32[4,8,32,1024]{3,2,1,0:T(8,128)} %x_ref.1, bf16[1024,128]{1,0:T(8,128)(2,1)} %constant.12.clone.fwd_high_hbm, bf16[1024,128]{1,0:T(8,128)(2,1)} %constant.13.clone.fwd_low_hbm, bf16[384,1024]{1,0:T(8,128)(2,1)} %constant.14.clone.back_hbm, ...), custom_call_target="tpu_custom_call" | custom-call | tf_op jit(solution)/shard_map/pallas_call | solution.py:776
  74.0 2.4 %shard_map.87 = (f32[4,8,32,1024]{3,2,1,0:T(8,128)}, f32[8,32,1024]{2,1,0:T(8,128)}) custom-call(f32[4,8,32,1024]{3,2,1,0:T(8,128)S(1)} %get-tuple-element.4.tend, f32[8,32,1024]{2,1,0:T(8,128)S(1)} %get-tuple-element.5.pot), custom_call_target="tpu_custom_call" | custom-call | tf_op jit(solution)/shard_map/pallas_call | solution.py:833

commit v5 on v4

--- a/solution.py
+++ b/solution.py
@@ -104,6 +104,44 @@
     out = [s * scaled - wave * j for s, j in zip(sums, jumps)]
     out[component] = out[component] + (sound_sq / 60.0) * sums[0]
     return out
+
+
+def radial_flux(r, n_rad, shells, at, start, out_at, ext, lo, hi, rowtab, tend, out, tile, carry):
+    step_r = radial_span / (n_rad * shells)
+    spot = pl.ds(at, ROWS)
+    lanes = pl.ds(pl.multiple_of(tile * LANES, LANES), LANES)
+    out_spot = pl.ds(out_at, ROWS)
+    out_lanes = pl.ds(pl.multiple_of((tile - start) * LANES, LANES), LANES)
+    sine = jnp.broadcast_to(rowtab[PADR + at : PADR + at + ROWS, 1:2], (ROWS, LANES)) * (
+        section_step / step_r
+    )
+
+    def cell(c, s):
+        if s < 0:
+            return lo[c, s + WIDTH, spot, lanes]
+        if s >= shells:
+            return hi[c, s - shells, spot, lanes]
+        return ext[c, s, pl.ds(PADR + at, ROWS), lanes]
+
+    u = [[cell(c, s) for s in range(-WIDTH, shells + WIDTH)] for c in range(4)]
+    last = None
+    for f in range(shells + 1):
+        place = r * shells + f
+        face_radius = inner_radius + step_r * place.astype(f32)
+        area = jnp.where((place > 0) & (place < n_rad * shells), face_radius * face_radius, 0.0)
+        sums, jumps = [], []
+        for c in range(4):
+            w = u[c][f : f + 6]
+            sums.append(37.0 * (w[2] + w[3]) - 8.0 * (w[1] + w[4]) + (w[0] + w[5]))
+            jumps.append(w[3] - w[2])
+        face = [value * area for value in flux(sums, jumps, 1)]
+        if f > 0:
+            for c in range(4):
+                out[c, f - 1, out_spot, out_lanes] = (
+                    section_step * tend[c, f - 1, spot, lanes] - (face[c] - last[c]) * sine
+                )
+        last = face
+    return carry
 
 
 def kernel(
@@ -124,6 +162,8 @@
     ext,
     lo,
     hi,
+    rowtab,
+    lead,
     relay,
     row_relay,
     fields,
@@ -132,7 +172,6 @@
     fwd_high_ref,
     fwd_low_ref,
     back_ref,
-    rowtab,
     degree_ref,
     log_ref,
     leg,
@@ -221,15 +260,15 @@
         return ((r // 2) * 2 + to % 2, y * 4 + (to // 2) * 2 + core)
 
     near = [
-        (None, along_x(1)),
-        (None, along_x(3)),
+        (x < 3, along_x(1)),
+        (x > 0, along_x(3)),
         (r + 2 < n_rad, (r + 2, a)),
         (r - 2 >= 0, (r - 2, a)),
         (a + 4 < n_ang, (r, a + 4)),
         (a - 4 >= 0, (r, a - 4)),
         (None, (r, a + 1 - 2 * core)),
     ]
-    n_near = 3
+    n_near = 1
     for cond, _ in near:
         if cond is not None:
             n_near = n_near + jnp.where(cond, 1, 0)
@@ -245,12 +284,16 @@
                 when(cond, signal)
 
     greet(barrier)
+    edge = pl.ds(jnp.where(even, shells - WIDTH, 0), WIDTH)
+    load_lead = pltpu.make_async_copy(
+        x_ref.at[:, edge, 0:ROWS, 0:wide], lead, local_sem.at[8]
+    )
+    load_lead.start()
     for load in (load_rows, load_degree, load_density, load_high, load_low):
         load.start()
     for load in (load_rest, load_log, load_back):
         load.start()
     pl.semaphore_wait(barrier, n_near)
-    greet(rounds.at[0])
 
     deep = shells // QUARTERS
     rows_up, rows_down, skip_up, skip_down, hand_up, hand_down = [], [], [], [], [], []
@@ -320,6 +363,14 @@
         when(c < n_up_far, far_up[c].start)
         when(c < n_down_far, far_down[c].start)
 
+    lead_to = pl.ds(0, ROWS), pl.ds(0, wide)
+    lead_up = remote(
+        lead, lo.at[:, :, *lead_to], rad_send.at[0, 0], rad_recv.at[0, 0], (r + 1, a)
+    )
+    lead_down = remote(
+        lead, hi.at[:, :, *lead_to], rad_send.at[1, 0], rad_recv.at[1, 0], (r - 1, a)
+    )
+
     def start_pair(c):
         when(even, rad_up[c].start)
         when(odd, rad_down[c].start)
@@ -343,7 +394,10 @@
             far_down[c].wait_recv()
             pass_down[c].start()
 
-    start_pair(0)
+    load_lead.wait()
+    when(even, lead_up.start)
+    when(odd, lead_down.start)
+    greet(rounds.at[0])
     for c in range(n_far):
         start_far(c)
     for c in range(QUARTERS - 1):
@@ -680,47 +734,13 @@
     for chunk in range(parts):
         when(r > 0, rad_up[chunk].wait_recv)
         when(r + 1 < n_rad, rad_down[chunk].wait_recv)
-        at = (chunk // CUTS) * ROWS
-        spot = pl.ds(at, ROWS)
-        first = (chunk % CUTS) * per
-
-        def radial_flux(tile, carry):
-            lanes = pl.ds(pl.multiple_of(tile * LANES, LANES), LANES)
-            sine = jnp.broadcast_to(
-                rowtab[PADR + at : PADR + at + ROWS, 1:2], (ROWS, LANES)
-            ) * (section_step / step_r)
-
-            def cell(c, s):
-                if s < 0:
-                    return lo[c, s + WIDTH, spot, lanes]
-                if s >= shells:
-                    return hi[c, s - shells, spot, lanes]
-                return ext[c, s, pl.ds(PADR + at, ROWS), lanes]
-
-            u = [[cell(c, s) for s in range(-WIDTH, shells + WIDTH)] for c in range(4)]
-            last = None
-            for f in range(shells + 1):
-                place = r * shells + f
-                face_radius = inner_radius + step_r * place.astype(f32)
-                area = jnp.where(
-                    (place > 0) & (place < n_rad * shells), face_radius * face_radius, 0.0
-                )
-                sums, jumps = [], []
-                for c in range(4):
-                    w = u[c][f : f + 6]
-                    sums.append(37.0 * (w[2] + w[3]) - 8.0 * (w[1] + w[4]) + (w[0] + w[5]))
-                    jumps.append(w[3] - w[2])
-                face = [value * area for value in flux(sums, jumps, 1)]
-                if f > 0:
-                    for c in range(4):
-                        tend[c, f - 1, spot, lanes] = (
-                            section_step * tend[c, f - 1, spot, lanes]
-                            - (face[c] - last[c]) * sine
-                        )
-                last = face
-            return carry
-
-        lax.fori_loop(first, first + per, radial_flux, 0)
+        if chunk < parts - 1:
+            at = (chunk // CUTS) * ROWS
+            first = (chunk % CUTS) * per
+            radial_tile = functools.partial(
+                radial_flux, r, n_rad, shells, at, 0, at, ext, lo, hi, rowtab, tend, tend
+            )
+            lax.fori_loop(first, first + per, radial_tile, 0)
 
     for c in range(QUARTERS):
         when(a + 1 < n_ang, rows_up[c].wait_send)
@@ -742,13 +762,35 @@
         when(r - 2 >= 0, hop_down(d).wait_send)
 
 
-def store(tend, pot, inc_ref, pot_ref, sem):
+def close(n_rad, tend, pot, ext, lo, hi, rowtab, inc_ref, pot_ref, final, sem):
+    _, shells, rows, cols = tend.shape
+    ahead = pl.ds(0, rows - ROWS)
+    behind = pl.ds(rows - ROWS, ROWS)
+    done = pl.ds(0, cols - cols // CUTS)
+    rest = pl.ds(cols - cols // CUTS, cols // CUTS)
     copies = [
-        pltpu.make_async_copy(tend.at[c], inc_ref.at[c], sem.at[c]) for c in range(tend.shape[0])
+        pltpu.make_async_copy(tend.at[c, :, ahead], inc_ref.at[c, :, ahead], sem.at[c])
+        for c in range(4)
     ]
-    copies.append(pltpu.make_async_copy(pot, pot_ref, sem.at[len(copies)]))
+    copies.append(
+        pltpu.make_async_copy(
+            tend.at[:, :, behind, done], inc_ref.at[:, :, behind, done], sem.at[4]
+        )
+    )
+    copies.append(pltpu.make_async_copy(pot, pot_ref, sem.at[5]))
     for copy in copies:
         copy.start()
+    r = lax.axis_index("rad")
+    tiles = cols // LANES
+    start = tiles - tiles // CUTS
+    radial_tile = functools.partial(
+        radial_flux, r, n_rad, shells, rows - ROWS, start, 0, ext, lo, hi, rowtab, tend, final
+    )
+    lax.fori_loop(start, tiles, radial_tile, 0)
+    copies.append(
+        pltpu.make_async_copy(final, inc_ref.at[:, :, behind, rest], sem.at[6])
+    )
+    copies[-1].start()
     for copy in copies:
         copy.wait()
 
@@ -773,18 +815,20 @@
         parts = (rows // ROWS) * CUTS
         inside = pl.BlockSpec(memory_space=pltpu.VMEM)
         dma = pltpu.SemaphoreType.DMA
-        increment, potential = pl.pallas_call(
+        results = pl.pallas_call(
             functools.partial(kernel, n_rad, n_ang, shells, rows, cols),
             out_shape=(
                 pltpu.VMEM(state.shape, f32),
                 pltpu.VMEM(state.shape[1:], f32),
-            ),
-            in_specs=[pl.BlockSpec(memory_space=pltpu.HBM)] * 7,
-            out_specs=(inside, inside),
-            scratch_shapes=[
                 pltpu.VMEM((4, shells, span, cols), f32),
                 pltpu.VMEM((4, WIDTH, rows, cols), f32),
                 pltpu.VMEM((4, WIDTH, rows, cols), f32),
+                pltpu.VMEM((span, LANES), f32),
+            ),
+            in_specs=[pl.BlockSpec(memory_space=pltpu.HBM)] * 7,
+            out_specs=(inside,) * 6,
+            scratch_shapes=[
+                pltpu.VMEM((4, WIDTH, ROWS, cols // CUTS), f32),
                 pltpu.VMEM((parts - CUTS, 4, WIDTH, ROWS, cols // CUTS), f32),
                 pltpu.VMEM((QUARTERS - 1, 4, shells // QUARTERS, WIDTH, cols), f32),
                 pltpu.VMEM((4 * rows, cols), f32),
@@ -793,7 +837,6 @@
                 pltpu.VMEM((cols, LANES), bf16),
                 pltpu.VMEM((cols, LANES), bf16),
                 pltpu.VMEM((3 * LANES, cols), bf16),
-                pltpu.VMEM((span, LANES), f32),
                 pltpu.VMEM((2 * NK + 8, LANES), f32),
                 pltpu.VMEM((shells, LANES), f32),
                 pltpu.VMEM((NK, span, LANES), f32),
@@ -807,7 +850,7 @@
                 pltpu.VMEM((n_rad // 2, 8, LANES), f32),
                 pltpu.VMEM((GROUPS, 2, KD, shells, LANES), f32),
                 pltpu.SemaphoreType.REGULAR((3,)),
-                dma((8,)),
+                dma((9,)),
                 dma((2, QUARTERS)),
                 dma((2, QUARTERS)),
                 dma((QUARTERS - 1,)),
@@ -826,21 +869,24 @@
                 dma((GROUPS,)),
             ],
             compiler_params=pltpu.CompilerParams(
-                collective_id=0, has_side_effects=True, vmem_limit_bytes=61_700_000
+                collective_id=0, has_side_effects=True, vmem_limit_bytes=52_200_000
             ),
         )(*operands)
         outside = pl.BlockSpec(memory_space=pltpu.HBM)
         return pl.pallas_call(
-            store,
+            functools.partial(close, n_rad),
             out_shape=(
                 jax.ShapeDtypeStruct(state.shape, f32),
                 jax.ShapeDtypeStruct(state.shape[1:], f32),
             ),
-            in_specs=(inside, inside),
+            in_specs=(inside,) * 6,
             out_specs=(outside, outside),
-            scratch_shapes=[dma((5,))],
-            compiler_params=pltpu.CompilerParams(vmem_limit_bytes=1 << 20),
-        )(increment, potential)
+            scratch_shapes=[
+                pltpu.VMEM((4, shells, ROWS, cols // CUTS), f32),
+                dma((7,)),
+            ],
+            compiler_params=pltpu.CompilerParams(vmem_limit_bytes=4 << 20),
+        )(*results)
 
     return jax.shard_map(
         body,

time: 77.5 us -> 76.2 us (0.983)
  no operation moved by 1% of the time
where the time goes in v5:
time: 76.2 us; the launch traced here: 75.8 us
  Pallas kernels  75.2 us (99%)
    pallas_call x1, Pallas kernels, body(): pl.pallas_call(functools.partial(kernel, n_rad, n_ang, shells, rows, cols...  72.7 us
    pallas_call x1, Pallas kernels, body(): pl.pallas_call(functools.partial(close, n_rad), out_shape=(jax.ShapeDtype...  2.41 us

profile of v5, /device:TPU:38, one launch (start us, length us, event | category | flops | bytes accessed | tf_op | source)
XLA Modules:
  0.0 75.8 jit_solution(710688053086596763)
XLA Ops:
  0.6 72.7 %shard_map.86 = (f32[4,8,32,1024]{3,2,1,0:T(8,128)S(1)}, f32[8,32,1024]{2,1,0:T(8,128)S(1)}, f32[4,8,48,1024]{3,2,1,0:T(8,128)S(1)}, f32[4,3,32,1024]{3,2,1,0:T(...) custom-call(f32[4,8,32,1024]{3,2,1,0:T(8,128)} %x_ref.1, ...), custom_call_target="tpu_custom_call" | custom-call | tf_op jit(solution)/shard_map/pallas_call | solution.py:818
  73.4 2.4 %shard_map.87 = (f32[4,8,32,1024]{3,2,1,0:T(8,128)}, f32[8,32,1024]{2,1,0:T(8,128)}) custom-call(f32[4,8,32,1024]{3,2,1,0:T(8,128)S(1)} %get-tuple-element.8.tend, f32[8,32,1024]{2,1,0:T(8,128)S(1)} %get-tuple-element.9.pot, f32[4,8,48,1024]{3,2,1,0:T(8,128)S(1)} %get-tuple-element.10.ext, f32[4,3,32,1024]{3,2,1,0:T(8,128)S(1)} %get-tuple-element.11.lo, ...), custom_call_target="tpu_custom_call" | custom-call | tf_op jit(solution)/shard_map/pallas_call | solution.py:876

commit v6 on v5

--- a/solution.py
+++ b/solution.py
@@ -346,8 +346,14 @@
         lo_part, hi_part = lo.at[:, :, part, band], hi.at[:, :, part, band]
         up_sems = rad_send.at[0, c], rad_recv.at[0, c]
         down_sems = rad_send.at[1, c], rad_recv.at[1, c]
-        rad_up.append(remote(above, lo_part, *up_sems, (r + 1, a)))
-        rad_down.append(remote(below, hi_part, *down_sems, (r - 1, a)))
+        if c < CUTS:
+            near_above, near_below = above, below
+        else:
+            held = pl.ds(PADR + (c // CUTS) * ROWS, ROWS)
+            near_above = ext.at[:, shells - WIDTH : shells, held, band]
+            near_below = ext.at[:, 0:WIDTH, held, band]
+        rad_up.append(remote(near_above, lo_part, *up_sems, (r + 1, a)))
+        rad_down.append(remote(near_below, hi_part, *down_sems, (r - 1, a)))
         if c < n_far:
             spot = relay.at[c]
             far_up.append(remote(above, spot, up_sems[0], far_recv.at[c], (r + 2, a)))
@@ -769,8 +775,10 @@
     done = pl.ds(0, cols - cols // CUTS)
     rest = pl.ds(cols - cols // CUTS, cols // CUTS)
     copies = [
-        pltpu.make_async_copy(tend.at[c, :, ahead], inc_ref.at[c, :, ahead], sem.at[c])
-        for c in range(4)
+        pltpu.make_async_copy(tend.at[c, half, ahead], inc_ref.at[c, half, ahead], sem.at[7 + k])
+        for k, (c, half) in enumerate(
+            (c, pl.ds(h * (shells // 2), shells // 2)) for c in range(4) for h in range(2)
+        )
     ]
     copies.append(
         pltpu.make_async_copy(
@@ -883,7 +891,7 @@
             out_specs=(outside, outside),
             scratch_shapes=[
                 pltpu.VMEM((4, shells, ROWS, cols // CUTS), f32),
-                dma((7,)),
+                dma((15,)),
             ],
             compiler_params=pltpu.CompilerParams(vmem_limit_bytes=4 << 20),
         )(*results)

time: 76.2 us -> 76.3 us (level)
  no operation moved by 1% of the time
where the time goes in v6:
time: 76.3 us; the launch traced here: 75.9 us
  Pallas kernels  75.2 us (99%)
    pallas_call x1, Pallas kernels, body(): pl.pallas_call(functools.partial(kernel, n_rad, n_ang, shells, rows, cols...  72.7 us
    pallas_call x1, Pallas kernels, body(): pl.pallas_call(functools.partial(close, n_rad), out_shape=(jax.ShapeDtype...  2.48 us

profile of v6, /device:TPU:38, one launch (start us, length us, event | category | flops | bytes accessed | tf_op | source)
XLA Modules:
  0.0 75.9 jit_solution(15708429105114862889)
XLA Ops:
  0.6 72.7 %shard_map.86 = (f32[4,8,32,1024]{3,2,1,0:T(8,128)S(1)}, f32[8,32,1024]{2,1,0:T(8,128)S(1)}, f32[4,8,48,1024]{3,2,1,0:T(8,128)S(1)}, f32[4,3,32,1024]{3,2,1,0:T(...) custom-call(f32[4,8,32,1024]{3,2,1,0:T(8,128)} %x_ref.1, ...), custom_call_target="tpu_custom_call" | custom-call | tf_op jit(solution)/shard_map/pallas_call | solution.py:826
  73.4 2.5 %shard_map.87 = (f32[4,8,32,1024]{3,2,1,0:T(8,128)}, f32[8,32,1024]{2,1,0:T(8,128)}) custom-call(f32[4,8,32,1024]{3,2,1,0:T(8,128)S(1)} %get-tuple-element.8.tend, f32[8,32,1024]{2,1,0:T(8,128)S(1)} %get-tuple-element.9.pot, f32[4,8,48,1024]{3,2,1,0:T(8,128)S(1)} %get-tuple-element.10.ext, f32[4,3,32,1024]{3,2,1,0:T(8,128)S(1)} %get-tuple-element.11.lo, ...), custom_call_target="tpu_custom_call" | custom-call | tf_op jit(solution)/shard_map/pallas_call | solution.py:884
